TPU v7x, 32 devices: a whole 2x2x4 slice. The times are simulated.
32 devices in a mesh: seq: 8 (over z, x), head: 4 (over y, core).
Axes of the slice: x: 2, y: 2, z: 4, core: 2. Of those that a mesh axis runs over, the one named last changes fastest.
Arguments:
- queries: float32 [16, 1024, 128], P('head', 'seq'), may hold values from -1.75 to 1.75
- keys: float32 [16, 1024, 128], P('head', 'seq'), may hold values from -1.75 to 1.75
- values: float32 [16, 1024, 128], P('head', 'seq'), may hold values from -10 to 10
- out_grad: float32 [16, 1024, 128], P('head', 'seq'), may hold values from -6 to 6
- norm_gain: float32 [16, 128], P('head'), may hold values from 0.1 to 1.9
- log_decay: float32 [16, 1024], P('head', 'seq'), may hold values from -1.5 to 0
- doc_ids: int32 [1024], P('seq'), may hold values from 0 to 7, never falling along the last dimension, each value on 1 to 512 neighbouring positions
Outputs:
- query_grad: float32 [16, 1024, 128], P('head', 'seq')
- key_grad: float32 [16, 1024, 128], P('head', 'seq')
- value_grad: float32 [16, 1024, 128], P('head', 'seq')
Inputs may be any that keep to these rules, and one draw needn't show every extreme that they name: `doc_ids`: document numbers never fall along the tokens; each document is 1 to 512 consecutive tokens, and one has exactly 512.
All inputs are finite; a program needn't handle non-finite values.
Results may differ from a plain program's by a relative error of at most 0.0003.
Values sent between devices are 32-bit elements; how exact they have to be, the bound alone decides.
A program may use at most 64 MiB of HBM per device.

v0:
```python
import jax
import jax.numpy as jnp
from jax import lax
from jax.sharding import PartitionSpec as P

HOPS = 4


EPSILON = 1e-06
PRECISE = lax.Precision.HIGHEST


def from_behind(array, axis, by):
    size = lax.axis_size(axis)
    pairs = [(i, i + by) for i in range(size) if 0 <= i + by < size]
    return lax.ppermute(array, axis, pairs)


def product(pattern, left_side, right_side):
    return jnp.einsum(
        pattern, left_side, right_side, precision=PRECISE, preferred_element_type=jnp.float32
    )


def join_forward(earlier, latter):
    early_state, early_pass, early_first, early_last = earlier
    late_state, late_pass, late_first, late_last = latter
    linked = (early_last == late_first) & (late_first == late_last) | (late_first <= 0.0)
    weight = jnp.where(linked, late_pass, 0.0)
    merged = late_state + weight[:, None, None] * early_state
    return (
        merged,
        early_pass * late_pass,
        jnp.where(early_first <= 0.0, late_first, early_first),
        jnp.where(late_last <= 0.0, early_last, late_last),
    )


def join_backward(upper_part, lower_part):
    high_state, high_pass, high_first, high_last = upper_part
    low_state, low_pass, low_first, low_last = lower_part
    linked = (low_last == high_first) & (low_first == low_last) | (low_first <= 0.0)
    weight = jnp.where(linked, low_pass, 0.0)
    merged = low_state + weight[:, None, None] * high_state
    return (
        merged,
        high_pass * low_pass,
        jnp.where(low_first <= 0.0, high_first, low_first),
        jnp.where(high_last <= 0.0, low_last, high_last),
    )


def per_device(queries, keys, values, out_grad, norm_gain, log_decay, doc_ids):
    head_count, tok_rows, head_width = queries.shape
    cumulative = jnp.cumsum(log_decay, axis=1)
    labels = doc_ids.astype(jnp.float32) + 1.0
    rows_iota = lax.broadcasted_iota(jnp.int32, (tok_rows, tok_rows), 0)
    cols_iota = lax.broadcasted_iota(jnp.int32, (tok_rows, tok_rows), 1)
    allowed = ((labels[:, None] == labels[None, :]) & (rows_iota >= cols_iota))[None]
    spread = cumulative[:, :, None] - cumulative[:, None, :]
    within = jnp.where(allowed, jnp.exp(jnp.where(allowed, spread, 0.0)), 0.0)
    scores = product("htd,hsd->hts", queries, keys)
    weighted = within * scores
    out_local = product("hts,hsd->htd", weighted, values)
    decay_tail = jnp.exp(cumulative[:, -1:] - cumulative)
    to_end = jnp.where((labels == labels[-1])[None, :], decay_tail, 0.0)
    kv_state = product("hsi,hsj->hij", keys * to_end[:, :, None], values)
    passing = jnp.exp(cumulative[:, -1])
    own_forward = (kv_state, passing, labels[0], labels[-1])
    carried = own_forward
    for repeat in range(HOPS):
        arrived = from_behind((carried[0], carried[1], carried[2], carried[3]), "seq", 1)
        if repeat + 1 < HOPS:
            carried = join_forward(arrived, own_forward)
    prior_state = arrived[0]
    from_prior = jnp.where((labels == arrived[3])[None, :], jnp.exp(cumulative), 0.0)
    attended = out_local + from_prior[:, :, None] * product("hti,hij->htj", queries, prior_state)
    scaled_grad = norm_gain[:, None, :] * out_grad
    totals = lax.psum(
        (jnp.sum(attended * attended, axis=(0, 2)), jnp.sum(scaled_grad * attended, axis=(0, 2))),
        "head",
    )
    width_all = head_count * head_width * lax.axis_size("head")
    inv_root = lax.rsqrt(totals[0] / width_all + EPSILON)
    coupling = totals[1] / width_all
    attn_grad = inv_root[None, :, None] * (
        scaled_grad - attended * (coupling * inv_root * inv_root)[None, :, None]
    )
    from_start = jnp.where((labels == labels[0])[None, :], jnp.exp(cumulative), 0.0)
    grad_state = product("hti,htj->hij", queries * from_start[:, :, None], attn_grad)
    own_backward = (grad_state, passing, labels[0], labels[-1])
    carried_back = own_backward
    for repeat in range(HOPS):
        arrived_back = from_behind(
            (carried_back[0], carried_back[1], carried_back[2], carried_back[3]), "seq", -1
        )
        if repeat + 1 < HOPS:
            carried_back = join_backward(arrived_back, own_backward)
    grad_weighted = within * product("htd,hsd->hts", attn_grad, values)
    query_grad = product("hts,hsd->htd", grad_weighted, keys)
    query_grad = query_grad + from_prior[:, :, None] * product(
        "htj,hij->hti", attn_grad, prior_state
    )
    key_local = product("hts,htd->hsd", grad_weighted, queries)
    value_local = product("hts,htd->hsd", weighted, attn_grad)
    later_state = arrived_back[0]
    to_next = jnp.where((labels == arrived_back[2])[None, :], decay_tail, 0.0)
    key_grad = key_local + to_next[:, :, None] * product("hij,hsj->hsi", later_state, values)
    value_grad = value_local + to_next[:, :, None] * product("hij,hsi->hsj", later_state, keys)
    return (query_grad, key_grad, value_grad)


def solution(mesh):
    in_specs = (
        P("head", "seq", None),
        P("head", "seq", None),
        P("head", "seq", None),
        P("head", "seq", None),
        P("head", None),
        P("head", "seq"),
        P("seq"),
    )
    out_specs = (P("head", "seq", None), P("head", "seq", None), P("head", "seq", None))
    return jax.shard_map(
        per_device, mesh=mesh, in_specs=in_specs, out_specs=out_specs, check_vma=False
    )
```

profile of v0, /device:TPU:0, one launch (start us, length us, event | category | flops | bytes accessed | tf_op | source)
XLA Modules:
  0.0 143.6 jit_solution(18398955665138103514)
XLA Ops:
  3.2 6.1 %collective-permute-start = (f32[]{:T(128)}, f32[]{:T(128)}, u32[]{:S(2)}, u32[]{:S(2)}) collective-permute-start(f32[]{:T(128)} %bitcast), channel_id=1, source_target_pairs={{0,4},{4,8},{8,12},{12,16},{16,20},{20,24},{24,28},{1,5},{5,9},{9,... | collective-permute-start | bytes 20 | tf_op jit(solution)/shard_map/ppermute | solution.py:16
  12.4 1.3 collective-permute-start.9
  15.1 7.4 %collective-permute-start.1 = (f32[]{:T(128)}, f32[]{:T(128)}, u32[]{:S(2)}, u32[]{:S(2)}) collective-permute-start(f32[]{:T(128)} %select_n.119), channel_id=1, source_target_pairs={{0,4},{4,8},{8,12},{12,16},{16,20},{20,24},{24,28},{1,5},{5,9},{9,... | collective-permute-start | bytes 20 | tf_op jit(solution)/shard_map/ppermute | solution.py:16
  23.8 1.3 collective-permute-start.10
  26.4 8.0 %collective-permute-start.2 = (f32[]{:T(128)}, f32[]{:T(128)}, u32[]{:S(2)}, u32[]{:S(2)}) collective-permute-start(f32[]{:T(128)} %select_n.120), channel_id=1, source_target_pairs={{0,4},{4,8},{8,12},{12,16},{16,20},{20,24},{24,28},{1,5},{5,9},{9,... | collective-permute-start | bytes 20 | tf_op jit(solution)/shard_map/ppermute | solution.py:16
  35.6 1.3 collective-permute-start.11
  38.2 8.0 %collective-permute-start.3 = (f32[]{:T(128)}, f32[]{:T(128)}, u32[]{:S(2)}, u32[]{:S(2)}) collective-permute-start(f32[]{:T(128)} %select_n.121), channel_id=1, source_target_pairs={{0,4},{4,8},{8,12},{12,16},{16,20},{20,24},{24,28},{1,5},{5,9},{9,... | collective-permute-start | bytes 20 | tf_op jit(solution)/shard_map/ppermute | solution.py:16
  46.2 2.6 %broadcast_compare_fusion.1 = (pred[128]{0:T(512)(128)(4,1)S(1)}, pred[128]{0:T(512)(128)(4,1)S(1)}, pred[128]{0:T(512)(128)(4,1)S(1)}, pred[128]{0:T(512)(128)(4,1)S(1)}) fusion(f32[]{:T(128)} %collective-permute-done.11, s32[128]{0:T(128)S(1)} %copy-done.6, f32[]{:T(128)} %bitcast.1, f32[]{:T(128)} %collective-permute-done.3, f32[]{:T(128)} %bitcast), kind=kLoop, calls=%fused_computation.44 | loop fusion | flops 768 | bytes 1040 | tf_op jit(solution)/shard_map/eq | solution.py:107
  48.8 1.6 %fusion.6 = f32[4,128,128]{2,1,0:T(8,128)S(1)} fusion(f32[4,128,128]{2,1,0:T(8,128)S(1)} %copy-done, f32[4,128,128]{2,1,0:T(8,128)} %param.8, f32[4,128]{1,0:T(4,128)S(1)} %get-tuple-element.9), kind=kOutput, calls=%fused_computation.21 | convolution fusion | flops 100728832 | bytes 788480 | tf_op jit(solution)/shard_map/hsi,hsj->hij/dot_general | solution.py:20
  50.4 4.8 %collective-permute-start.4 = (f32[4,128,128]{2,1,0:T(8,128)S(1)}, f32[4,128,128]{2,1,0:T(8,128)S(1)}, u32[]{:S(2)}, u32[]{:S(2)}) collective-permute-start(f32[4,128,128]{2,1,0:T(8,128)S(1)} %fusion.6), channel_id=1, source_target_pairs={{0,4},{4,8},{8,12},{12,16},{16,20},{20,24},{24,28},{1,5},{5,9},{9,... | collective-permute-start | bytes 786440 | tf_op jit(solution)/shard_map/ppermute | solution.py:16
  64.3 5.0 %collective-permute-start.5 = (f32[4,128,128]{2,1,0:T(8,128)S(1)}, f32[4,128,128]{2,1,0:T(8,128)S(1)}, u32[]{:S(2)}, u32[]{:S(2)}) collective-permute-start(f32[4,128,128]{2,1,0:T(8,128)S(1)} %multiply_add_fusion.6), channel_id=1, source_target_pairs={{0,4},{4,8},{8,12},{12,16},{16,20},{20,24},{24,28},{1,5},{5,9},{9,... | collective-permute-start | bytes 786440 | tf_op jit(solution)/shard_map/ppermute | solution.py:16
  69.4 6.7 %collective-permute-done.5 = f32[4,128,128]{2,1,0:T(8,128)S(1)} collective-permute-done((f32[4,128,128]{2,1,0:T(8,128)S(1)}, f32[4,128,128]{2,1,0:T(8,128)S(1)}, u32[]{:S(2)}, u32[]{:S(2)}) %collective-permute-start.5) | collective-permute-done | bytes 262176 | tf_op jit(solution)/shard_map/ppermute | solution.py:16
  76.1 4.4 %collective-permute-start.6 = (f32[4,128,128]{2,1,0:T(8,128)S(1)}, f32[4,128,128]{2,1,0:T(8,128)S(1)}, u32[]{:S(2)}, u32[]{:S(2)}) collective-permute-start(f32[4,128,128]{2,1,0:T(8,128)S(1)} %multiply_add_fusion.5), channel_id=1, source_target_pairs={{0,4},{4,8},{8,12},{12,16},{16,20},{20,24},{24,28},{1,5},{5,9},{9,... | collective-permute-start | bytes 786440 | tf_op jit(solution)/shard_map/ppermute | solution.py:16
  80.6 5.8 %collective-permute-done.6 = f32[4,128,128]{2,1,0:T(8,128)S(1)} collective-permute-done((f32[4,128,128]{2,1,0:T(8,128)S(1)}, f32[4,128,128]{2,1,0:T(8,128)S(1)}, u32[]{:S(2)}, u32[]{:S(2)}) %collective-permute-start.6) | collective-permute-done | bytes 262176 | tf_op jit(solution)/shard_map/ppermute | solution.py:16
  86.6 4.5 %collective-permute-start.7 = (f32[4,128,128]{2,1,0:T(8,128)S(1)}, f32[4,128,128]{2,1,0:T(8,128)S(1)}, u32[]{:S(2)}, u32[]{:S(2)}) collective-permute-start(f32[4,128,128]{2,1,0:T(8,128)S(1)} %multiply_add_fusion.4), channel_id=1, source_target_pairs={{0,4},{4,8},{8,12},{12,16},{16,20},{20,24},{24,28},{1,5},{5,9},{9,... | collective-permute-start | bytes 786440 | tf_op jit(solution)/shard_map/ppermute | solution.py:16
  92.5 2.4 %collective-permute-done.7 = f32[4,128,128]{2,1,0:T(8,128)S(1)} collective-permute-done((f32[4,128,128]{2,1,0:T(8,128)S(1)}, f32[4,128,128]{2,1,0:T(8,128)S(1)}, u32[]{:S(2)}, u32[]{:S(2)}) %collective-permute-start.7) | collective-permute-done | bytes 262176 | tf_op jit(solution)/shard_map/ppermute | solution.py:16
  95.6 5.7 %all-reduce = (f32[128]{0:T(128)S(1)}, f32[128]{0:T(128)S(1)}) all-reduce(f32[128]{0:T(128)S(1)} %get-tuple-element.4, f32[128]{0:T(128)S(1)} %get-tuple-element.3), channel_id=1, replica_groups=mesh['seq'=8,'head'=4] {'head'}, use_global_device_ids=true, to_apply=%region_4.5 | all-reduce | flops 256 | bytes 2048 | tf_op jit(solution)/shard_map/psum | solution.py:79
  103.4 9.4 %collective-permute-done.12 = f32[4,128,128]{2,1,0:T(8,128)S(1)} collective-permute-done((f32[4,128,128]{2,1,0:T(8,128)S(1)}, f32[4,128,128]{2,1,0:T(8,128)S(1)}, u32[]{:S(2)}, u32[]{:S(2)}) %collective-permute-start.12) | collective-permute-done | bytes 262176 | tf_op jit(solution)/shard_map/ppermute | solution.py:16
  114.8 8.1 %collective-permute-done.13 = f32[4,128,128]{2,1,0:T(8,128)S(1)} collective-permute-done((f32[4,128,128]{2,1,0:T(8,128)S(1)}, f32[4,128,128]{2,1,0:T(8,128)S(1)}, u32[]{:S(2)}, u32[]{:S(2)}) %collective-permute-start.13) | collective-permute-done | bytes 262176 | tf_op jit(solution)/shard_map/ppermute | solution.py:16
  123.0 1.3 collective-permute-start.14
  125.6 6.6 %collective-permute-done.14 = f32[4,128,128]{2,1,0:T(8,128)S(1)} collective-permute-done((f32[4,128,128]{2,1,0:T(8,128)S(1)}, f32[4,128,128]{2,1,0:T(8,128)S(1)}, u32[]{:S(2)}, u32[]{:S(2)}) %collective-permute-start.14) | collective-permute-done | bytes 262176 | tf_op jit(solution)/shard_map/ppermute | solution.py:16
  134.0 1.3 multiply_add_fusion.3
  135.3 5.9 %collective-permute-done.15 = f32[4,128,128]{2,1,0:T(8,128)S(1)} collective-permute-done((f32[4,128,128]{2,1,0:T(8,128)S(1)}, f32[4,128,128]{2,1,0:T(8,128)S(1)}, u32[]{:S(2)}, u32[]{:S(2)}) %collective-permute-start.15) | collective-permute-done | bytes 262176 | tf_op jit(solution)/shard_map/ppermute | solution.py:16
  142.3 1.4 fusion.3
  (52 shorter events, 13.9 us)
Async XLA Ops:
  0.6 48.2 %copy-start = (f32[4,128,128]{2,1,0:T(8,128)S(1)}, f32[4,128,128]{2,1,0:T(8,128)}, u32[]{:S(2)}) copy-start(f32[4,128,128]{2,1,0:T(8,128)} %param.9) | copy-start | bytes 786436
  1.9 9.2 %collective-permute-start.8 = (f32[]{:T(128)}, f32[]{:T(128)}, u32[]{:S(2)}, u32[]{:S(2)}) collective-permute-start(f32[]{:T(128)} %bitcast.1), channel_id=1, source_target_pairs={{4,0},{8,4},{12,8},{16,12},{20,16},{24,20},{28,24},{5,1},{9,5},{13... | collective-permute-start | bytes 20 | tf_op jit(solution)/shard_map/ppermute | solution.py:16
  3.2 7.4 %copy-start.5 = (f32[4,128]{1,0:T(4,128)S(1)}, f32[4,128]{1,0:T(4,128)}, u32[]{:S(2)}) copy-start(f32[4,128]{1,0:T(4,128)} %param.12) | copy-start | bytes 6148
  3.2 10.5 %collective-permute-start = (f32[]{:T(128)}, f32[]{:T(128)}, u32[]{:S(2)}, u32[]{:S(2)}) collective-permute-start(f32[]{:T(128)} %bitcast), channel_id=1, source_target_pairs={{0,4},{4,8},{8,12},{12,16},{16,20},{20,24},{24,28},{1,5},{5,9},{9,... | collective-permute-start | bytes 20 | tf_op jit(solution)/shard_map/ppermute | solution.py:16
  12.4 10.1 %collective-permute-start.9 = (f32[]{:T(128)}, f32[]{:T(128)}, u32[]{:S(2)}, u32[]{:S(2)}) collective-permute-start(f32[]{:T(128)} %select_n.130), channel_id=1, source_target_pairs={{4,0},{8,4},{12,8},{16,12},{20,16},{24,20},{28,24},{5,1},{9,5},{13... | collective-permute-start | bytes 20 | tf_op jit(solution)/shard_map/ppermute | solution.py:16
  15.1 10.0 %collective-permute-start.1 = (f32[]{:T(128)}, f32[]{:T(128)}, u32[]{:S(2)}, u32[]{:S(2)}) collective-permute-start(f32[]{:T(128)} %select_n.119), channel_id=1, source_target_pairs={{0,4},{4,8},{8,12},{12,16},{16,20},{20,24},{24,28},{1,5},{5,9},{9,... | collective-permute-start | bytes 20 | tf_op jit(solution)/shard_map/ppermute | solution.py:16
  23.8 10.7 %collective-permute-start.10 = (f32[]{:T(128)}, f32[]{:T(128)}, u32[]{:S(2)}, u32[]{:S(2)}) collective-permute-start(f32[]{:T(128)} %select_n.131), channel_id=1, source_target_pairs={{4,0},{8,4},{12,8},{16,12},{20,16},{24,20},{28,24},{5,1},{9,5},{13... | collective-permute-start | bytes 20 | tf_op jit(solution)/shard_map/ppermute | solution.py:16
  26.4 10.5 %collective-permute-start.2 = (f32[]{:T(128)}, f32[]{:T(128)}, u32[]{:S(2)}, u32[]{:S(2)}) collective-permute-start(f32[]{:T(128)} %select_n.120), channel_id=1, source_target_pairs={{0,4},{4,8},{8,12},{12,16},{16,20},{20,24},{24,28},{1,5},{5,9},{9,... | collective-permute-start | bytes 20 | tf_op jit(solution)/shard_map/ppermute | solution.py:16
  35.6 10.5 %copy-start.6 = (s32[128]{0:T(128)S(1)}, s32[128]{0:T(128)}, u32[]{:S(2)}) copy-start(s32[128]{0:T(128)} %param.13) | copy-start | bytes 1540
  35.6 10.5 %collective-permute-start.11 = (f32[]{:T(128)}, f32[]{:T(128)}, u32[]{:S(2)}, u32[]{:S(2)}) collective-permute-start(f32[]{:T(128)} %select_n.132), channel_id=1, source_target_pairs={{4,0},{8,4},{12,8},{16,12},{20,16},{24,20},{28,24},{5,1},{9,5},{13... | collective-permute-start | bytes 20 | tf_op jit(solution)/shard_map/ppermute | solution.py:16
  38.2 8.0 %collective-permute-start.3 = (f32[]{:T(128)}, f32[]{:T(128)}, u32[]{:S(2)}, u32[]{:S(2)}) collective-permute-start(f32[]{:T(128)} %select_n.121), channel_id=1, source_target_pairs={{0,4},{4,8},{8,12},{12,16},{16,20},{20,24},{24,28},{1,5},{5,9},{9,... | collective-permute-start | bytes 20 | tf_op jit(solution)/shard_map/ppermute | solution.py:16
  50.4 13.8 %collective-permute-start.4 = (f32[4,128,128]{2,1,0:T(8,128)S(1)}, f32[4,128,128]{2,1,0:T(8,128)S(1)}, u32[]{:S(2)}, u32[]{:S(2)}) collective-permute-start(f32[4,128,128]{2,1,0:T(8,128)S(1)} %fusion.6), channel_id=1, source_target_pairs={{0,4},{4,8},{8,12},{12,16},{16,20},{20,24},{24,28},{1,5},{5,9},{9,... | collective-permute-start | bytes 786440 | tf_op jit(solution)/shard_map/ppermute | solution.py:16
  64.3 11.7 %collective-permute-start.5 = (f32[4,128,128]{2,1,0:T(8,128)S(1)}, f32[4,128,128]{2,1,0:T(8,128)S(1)}, u32[]{:S(2)}, u32[]{:S(2)}) collective-permute-start(f32[4,128,128]{2,1,0:T(8,128)S(1)} %multiply_add_fusion.6), channel_id=1, source_target_pairs={{0,4},{4,8},{8,12},{12,16},{16,20},{20,24},{24,28},{1,5},{5,9},{9,... | collective-permute-start | bytes 786440 | tf_op jit(solution)/shard_map/ppermute | solution.py:16
  76.1 10.3 %collective-permute-start.6 = (f32[4,128,128]{2,1,0:T(8,128)S(1)}, f32[4,128,128]{2,1,0:T(8,128)S(1)}, u32[]{:S(2)}, u32[]{:S(2)}) collective-permute-start(f32[4,128,128]{2,1,0:T(8,128)S(1)} %multiply_add_fusion.5), channel_id=1, source_target_pairs={{0,4},{4,8},{8,12},{12,16},{16,20},{20,24},{24,28},{1,5},{5,9},{9,... | collective-permute-start | bytes 786440 | tf_op jit(solution)/shard_map/ppermute | solution.py:16
  86.5 4.7 %copy-start.1 = (f32[4,128,128]{2,1,0:T(8,128)S(1)}, f32[4,128,128]{2,1,0:T(8,128)}, u32[]{:S(2)}) copy-start(f32[4,128,128]{2,1,0:T(8,128)} %param.7) | copy-start | bytes 786436
  86.5 4.7 %copy-start.2 = (f32[4,128,128]{2,1,0:T(8,128)S(1)}, f32[4,128,128]{2,1,0:T(8,128)}, u32[]{:S(2)}) copy-start(f32[4,128,128]{2,1,0:T(8,128)} %param.8) | copy-start | bytes 786436
  86.5 5.2 %copy-start.3 = (f32[4,128,128]{2,1,0:T(8,128)S(1)}, f32[4,128,128]{2,1,0:T(8,128)}, u32[]{:S(2)}) copy-start(f32[4,128,128]{2,1,0:T(8,128)} %param.10) | copy-start | bytes 786436
  86.6 8.4 %collective-permute-start.7 = (f32[4,128,128]{2,1,0:T(8,128)S(1)}, f32[4,128,128]{2,1,0:T(8,128)S(1)}, u32[]{:S(2)}, u32[]{:S(2)}) collective-permute-start(f32[4,128,128]{2,1,0:T(8,128)S(1)} %multiply_add_fusion.4), channel_id=1, source_target_pairs={{0,4},{4,8},{8,12},{12,16},{16,20},{20,24},{24,28},{1,5},{5,9},{9,... | collective-permute-start | bytes 786440 | tf_op jit(solution)/shard_map/ppermute | solution.py:16
  91.9 3.0 %copy-start.4 = (f32[4,128]{1,0:T(4,128)S(1)}, f32[4,128]{1,0:T(4,128)}, u32[]{:S(2)}) copy-start(f32[4,128]{1,0:T(4,128)} %param.11) | copy-start | bytes 6148
  102.1 10.7 %collective-permute-start.12 = (f32[4,128,128]{2,1,0:T(8,128)S(1)}, f32[4,128,128]{2,1,0:T(8,128)S(1)}, u32[]{:S(2)}, u32[]{:S(2)}) collective-permute-start(f32[4,128,128]{2,1,0:T(8,128)S(1)} %fusion.4), channel_id=1, source_target_pairs={{4,0},{8,4},{12,8},{16,12},{20,16},{24,20},{28,24},{5,1},{9,5},{13... | collective-permute-start | bytes 786440 | tf_op jit(solution)/shard_map/ppermute | solution.py:16
  112.9 10.0 %collective-permute-start.13 = (f32[4,128,128]{2,1,0:T(8,128)S(1)}, f32[4,128,128]{2,1,0:T(8,128)S(1)}, u32[]{:S(2)}, u32[]{:S(2)}) collective-permute-start(f32[4,128,128]{2,1,0:T(8,128)S(1)} %multiply_add_fusion.2), channel_id=1, source_target_pairs={{4,0},{8,4},{12,8},{16,12},{20,16},{24,20},{28,24},{5,1},{9,5},{13... | collective-permute-start | bytes 786440 | tf_op jit(solution)/shard_map/ppermute | solution.py:16
  123.0 9.2 %collective-permute-start.14 = (f32[4,128,128]{2,1,0:T(8,128)S(1)}, f32[4,128,128]{2,1,0:T(8,128)S(1)}, u32[]{:S(2)}, u32[]{:S(2)}) collective-permute-start(f32[4,128,128]{2,1,0:T(8,128)S(1)} %multiply_add_fusion.1), channel_id=1, source_target_pairs={{4,0},{8,4},{12,8},{16,12},{20,16},{24,20},{28,24},{5,1},{9,5},{13... | collective-permute-start | bytes 786440 | tf_op jit(solution)/shard_map/ppermute | solution.py:16
  132.3 8.9 %collective-permute-start.15 = (f32[4,128,128]{2,1,0:T(8,128)S(1)}, f32[4,128,128]{2,1,0:T(8,128)S(1)}, u32[]{:S(2)}, u32[]{:S(2)}) collective-permute-start(f32[4,128,128]{2,1,0:T(8,128)S(1)} %multiply_add_fusion), channel_id=1, source_target_pairs={{4,0},{8,4},{12,8},{16,12},{20,16},{24,20},{28,24},{5,1},{9,5},{13... | collective-permute-start | bytes 786440 | tf_op jit(solution)/shard_map/ppermute | solution.py:16
where the time goes:
time: 145 us; the launch traced here: 144 us
  starting transfers between devices  58.6 us (40%)
  waiting for transfers between devices  44.9 us (31%)
  between operations  18.8 us (13%)
  matrix products  10.2 us (7%)
  blocking collectives  5.66 us (4%)
  other arithmetic  4.45 us (3%)
    ppermute x16, starting transfers between devices, from_behind(): return lax.ppermute(array, axis, pairs)  58.6 us
    ppermute x16, waiting for transfers between devices, from_behind(): return lax.ppermute(array, axis, pairs)  44.9 us
    dot_general x12, matrix products, product(): jnp.einsum(pattern, left_side, right_side, precision=PRECISE, preferred_e...  10.2 us
    psum x1, blocking collectives, per_device(): lax.psum((jnp.sum(attended * attended, axis=(0, 2)), jnp.sum(scaled_grad...  5.66 us
  transfers between devices with their start and end apart: 16, of which 7 were waited for; matrix products, arithmetic and copies ran while one was open for 4% of the time, Pallas kernels for 0%

commit v1 on v0

v1 whole, which is shorter than its diff:
```python
import functools
import jax
import jax.numpy as jnp
from jax import lax
from jax.experimental import pallas as pl
from jax.experimental.pallas import tpu as pltpu
from jax.sharding import PartitionSpec as P

EPSILON = 1e-06
F32 = jnp.float32
NN = (((1,), (0,)), ((), ()))
NT = (((1,), (1,)), ((), ()))
MESH = pl.DeviceIdType.MESH


def split(x):
    hi = x.astype(jnp.bfloat16)
    lo = (x - hi.astype(F32)).astype(jnp.bfloat16)
    return hi, lo


def mm(a, b, dims):
    def one(x, y):
        return lax.dot_general(x, y, dims, preferred_element_type=F32)

    return one(a[0], b[0]) + (one(a[0], b[1]) + one(a[1], b[0]))


def body(n, hs, q, k, v, og, gain, ld, doc, dq, dk, dv,
         own_f, pair_f, w_f, a_f, b_f, own_b, pair_b, w_b, a_b, b_b,
         att, wgt, wth, prior, ags, tot, send, recv, psend, precv):
    heads, rows, width = q.shape
    s = lax.axis_index("seq")
    hd = lax.axis_index("head")
    odd_i = lax.rem(s, 2)
    partner = s + 1 - 2 * odd_i
    odd = odd_i.astype(F32)
    even = 1.0 - odd
    has_up = s >= 2
    has_down = s < n - 2

    barrier = pltpu.get_barrier_semaphore()
    pl.semaphore_signal(barrier, inc=1, device_id={"seq": partner}, device_id_type=MESH)
    for j in range(1, hs):
        pl.semaphore_signal(barrier, inc=1, device_id={"head": lax.rem(hd + j, hs)}, device_id_type=MESH)

    @pl.when(has_up)
    def _():
        pl.semaphore_signal(barrier, inc=1, device_id={"seq": s - 2}, device_id_type=MESH)

    @pl.when(has_down)
    def _():
        pl.semaphore_signal(barrier, inc=1, device_id={"seq": s + 2}, device_id_type=MESH)

    def copy(kind, h, src, dst, to):
        return pltpu.make_async_remote_copy(
            src_ref=src.at[h], dst_ref=dst.at[h], send_sem=send.at[kind, h],
            recv_sem=recv.at[kind, h], device_id={"seq": to}, device_id_type=MESH)

    def x_f(h):
        return copy(0, h, own_f, pair_f, partner)

    def c_a(h):
        return copy(1, h, w_f, a_f, s + 2)

    def c_b(h):
        return copy(2, h, a_f, b_f, s + 2)

    def x_b(h):
        return copy(3, h, own_b, pair_b, partner)

    def d_a(h):
        return copy(4, h, w_b, a_b, s - 2)

    def d_b(h):
        return copy(5, h, a_b, b_b, s - 2)

    ri = lax.broadcasted_iota(jnp.int32, (rows, rows), 0)
    ci = lax.broadcasted_iota(jnp.int32, (rows, rows), 1)
    tri = jnp.where(ri <= ci, 1.0, 0.0)
    cum = lax.dot_general(ld[...], tri, NN, precision=lax.Precision.HIGHEST, preferred_element_type=F32)
    lab = doc[...].astype(F32) + 1.0
    first = jnp.broadcast_to(lab[:, 0:1], (1, width))
    last = jnp.broadcast_to(lab[:, rows - 1:rows], (1, width))
    mi = lax.broadcasted_iota(jnp.int32, (8, width), 0)

    def meta(passing, first_row, last_row):
        return jnp.where(mi == 0, passing, jnp.where(mi == 1, first_row, last_row))

    def parts(buf, h):
        return (buf[h, rows:rows + 1, :], buf[h, rows + 1:rows + 2, :], buf[h, rows + 2:rows + 3, :])

    def row(h):
        return cum[h:h + 1, :]

    def total(h):
        return cum[h:h + 1, rows - 1:rows]

    def passing(h):
        return jnp.broadcast_to(jnp.exp(total(h)), (1, width))

    def column(r):
        return jnp.broadcast_to(r, (width, r.shape[1])).T

    def put(buf, h, state):
        buf[h, 0:width, :] = state
        buf[h, width:width + 8, :] = meta(passing(h), first, last)

    for h in range(heads):
        tail = jnp.where(lab == last[:, 0:1], jnp.exp(total(h) - row(h)), 0.0)
        put(own_f, h, mm(split(k[h].T * tail), split(v[h]), NN))
        if h == 0:
            count = hs + has_up.astype(jnp.int32) + has_down.astype(jnp.int32)
            pl.semaphore_wait(barrier, count)
        x_f(h).start()

    @pl.when(s < 2)
    def _():
        a_f[...] = jnp.zeros_like(a_f)

    @pl.when(s < 4)
    def _():
        b_f[...] = jnp.zeros_like(b_f)

    @pl.when(s >= n - 2)
    def _():
        a_b[...] = jnp.zeros_like(a_b)

    @pl.when(s >= n - 4)
    def _():
        b_b[...] = jnp.zeros_like(b_b)

    lab_col = column(lab)
    allowed = (lab_col == lab) & (ri >= ci)

    def local_forward(h):
        spread = column(row(h)) - row(h)
        within = jnp.where(allowed, jnp.exp(jnp.where(allowed, spread, 0.0)), 0.0)
        wth[h] = within
        weighted = within * mm(split(q[h]), split(k[h]), NT)
        wgt[h] = weighted
        att[h] = mm(split(weighted), split(v[h]), NN)

    def merge_forward(h):
        x_f(h).wait_recv()
        p_pass, p_first, p_last = parts(pair_f, h)
        o_pass = passing(h)
        w_even = jnp.where((last == p_first) & (p_first == p_last), p_pass, 0.0)
        w_odd = jnp.where((p_last == first) & (first == last), o_pass, 0.0)
        c_own = odd + even * w_even
        c_pair = even + odd * w_odd
        w_f[h, 0:width, :] = c_own * own_f[h, 0:width, :] + c_pair * pair_f[h, 0:width, :]
        w_f[h, width:width + 8, :] = meta(
            o_pass * p_pass, even * first + odd * p_first, odd * last + even * p_last)

        @pl.when(has_down)
        def _():
            c_a(h).start()

    def relay_forward(h):
        @pl.when(has_up)
        def _():
            c_a(h).wait_recv()

        @pl.when(has_up & has_down)
        def _():
            c_b(h).start()

    def finish_forward(h):
        @pl.when(s >= 4)
        def _():
            c_b(h).wait_recv()

        a_pass, a_first, a_last = parts(a_f, h)
        b_last = parts(b_f, h)[2]
        p_pass, p_first, p_last = parts(pair_f, h)
        join = jnp.where((b_last == a_first) & (a_first == a_last), a_pass, 0.0)
        step = jnp.where((a_last == p_first) & (p_first == p_last), p_pass, 0.0)
        base = a_f[h, 0:width, :] + join * b_f[h, 0:width, :]
        state = (even + odd * step) * base + odd * pair_f[h, 0:width, :]
        prior[h] = state
        label = even * a_last + odd * p_last
        from_prior = column(jnp.where(lab == label, jnp.exp(row(h)), 0.0))
        attended = att[h] + from_prior * mm(split(q[h]), split(state), NN)
        att[h] = attended
        scaled = gain[h:h + 1, :] * og[h]
        return attended * attended, scaled * attended

    half = heads // 2
    for h in range(half):
        local_forward(h)
    for h in range(heads):
        merge_forward(h)
    for h in range(half, heads):
        local_forward(h)
    for h in range(heads):
        relay_forward(h)
    squares, inner = None, None
    for h in range(heads):
        one, two = finish_forward(h)
        squares = one if h == 0 else squares + one
        inner = two if h == 0 else inner + two
    sum_sq = jnp.sum(squares.T, axis=0, keepdims=True)
    sum_in = jnp.sum(inner.T, axis=0, keepdims=True)
    tot[0] = jnp.where(mi == 0, sum_sq, sum_in)

    def peer(j):
        return pltpu.make_async_remote_copy(
            src_ref=tot.at[0], dst_ref=tot.at[j], send_sem=psend.at[j], recv_sem=precv.at[j],
            device_id={"head": lax.rem(hd + j, hs)}, device_id_type=MESH)

    for j in range(1, hs):
        peer(j).start()
    for j in range(1, hs):
        peer(j).wait_recv()
    totals = tot[0]
    for j in range(1, hs):
        totals = totals + tot[j]
    width_all = heads * width * hs
    inv_row = lax.rsqrt(totals[0:1, :] / width_all + EPSILON)
    cpl_row = totals[1:2, :] / width_all * inv_row * inv_row
    inv_col = column(inv_row)
    cpl_col = column(cpl_row)

    for h in range(heads):
        grad = inv_col * (gain[h:h + 1, :] * og[h] - att[h] * cpl_col)
        ags[h] = grad
        from_start = jnp.where(lab == first[:, 0:1], jnp.exp(row(h)), 0.0)
        put(own_b, h, mm(split(q[h].T * from_start), split(grad), NN))
        x_b(h).start()

    def local_backward(h):
        grad = split(ags[h])
        gw = wth[h] * mm(grad, split(v[h]), NT)
        p_last = parts(pair_f, h)[2]
        label = even * parts(a_f, h)[2] + odd * p_last
        from_prior = column(jnp.where(lab == label, jnp.exp(row(h)), 0.0))
        dq[h] = mm(split(gw), split(k[h]), NN) + from_prior * mm(grad, split(prior[h]), NT)
        dk[h] = mm(split(gw.T), split(q[h]), NN)
        dv[h] = mm(split(wgt[h].T), grad, NN)

    def merge_backward(h):
        x_b(h).wait_recv()
        p_pass, p_first, p_last = parts(pair_b, h)
        o_pass = passing(h)
        w_even = jnp.where((last == p_first) & (first == last), o_pass, 0.0)
        w_odd = jnp.where((p_last == first) & (p_first == p_last), p_pass, 0.0)
        c_own = even + odd * w_odd
        c_pair = odd + even * w_even
        w_b[h, 0:width, :] = c_own * own_b[h, 0:width, :] + c_pair * pair_b[h, 0:width, :]
        w_b[h, width:width + 8, :] = meta(
            o_pass * p_pass, even * first + odd * p_first, odd * last + even * p_last)

        @pl.when(has_up)
        def _():
            d_a(h).start()

    def relay_backward(h):
        @pl.when(has_down)
        def _():
            d_a(h).wait_recv()

        @pl.when(has_up & has_down)
        def _():
            d_b(h).start()

    def finish_backward(h):
        @pl.when(s < n - 4)
        def _():
            d_b(h).wait_recv()

        a_pass, a_first, a_last = parts(a_b, h)
        b_first = parts(b_b, h)[1]
        p_pass, p_first, p_last = parts(pair_b, h)
        join = jnp.where((a_last == b_first) & (a_first == a_last), a_pass, 0.0)
        step = jnp.where((p_last == a_first) & (p_first == p_last), p_pass, 0.0)
        base = a_b[h, 0:width, :] + join * b_b[h, 0:width, :]
        state = split((odd + even * step) * base + even * pair_b[h, 0:width, :])
        label = odd * a_first + even * p_first
        to_next = column(jnp.where(lab == label, jnp.exp(total(h) - row(h)), 0.0))
        dk[h] = dk[h] + to_next * mm(split(v[h]), state, NT)
        dv[h] = dv[h] + to_next * mm(split(k[h]), state, NN)

    for h in range(half):
        local_backward(h)
    for h in range(heads):
        merge_backward(h)
    for h in range(half, heads):
        local_backward(h)
    for h in range(heads):
        relay_backward(h)
    for h in range(heads):
        finish_backward(h)

    for j in range(1, hs):
        peer(j).wait_send()
    for h in range(heads):
        x_f(h).wait_send()
        x_b(h).wait_send()

        @pl.when(has_down)
        def _():
            c_a(h).wait_send()

        @pl.when(has_up)
        def _():
            d_a(h).wait_send()

        @pl.when(has_up & has_down)
        def _():
            c_b(h).wait_send()
            d_b(h).wait_send()


def per_device(queries, keys, values, out_grad, norm_gain, log_decay, doc_ids):
    n, hs = lax.axis_size("seq"), lax.axis_size("head")
    heads, rows, width = queries.shape
    whole = pl.BlockSpec(memory_space=pltpu.VMEM)
    state = pltpu.VMEM((heads, width + 8, width), F32)
    square = pltpu.VMEM((heads, rows, width), F32)
    scores = pltpu.VMEM((heads, rows, rows), F32)
    out = jax.ShapeDtypeStruct(queries.shape, F32)
    return pl.pallas_call(
        functools.partial(body, n, hs),
        out_shape=(out, out, out),
        in_specs=[whole] * 7,
        out_specs=(whole, whole, whole),
        scratch_shapes=[state] * 10 + [
            square, scores, scores, pltpu.VMEM((heads, width, width), F32), square,
            pltpu.VMEM((hs, 8, rows), F32),
            pltpu.SemaphoreType.DMA((6, heads)), pltpu.SemaphoreType.DMA((6, heads)),
            pltpu.SemaphoreType.DMA((hs,)), pltpu.SemaphoreType.DMA((hs,)),
        ],
        compiler_params=pltpu.CompilerParams(
            collective_id=0, has_side_effects=True, vmem_limit_bytes=32 * 1024 * 1024),
    )(queries, keys, values, out_grad, norm_gain, log_decay, doc_ids[None, :])


def solution(mesh):
    in_specs = (
        P("head", "seq", None),
        P("head", "seq", None),
        P("head", "seq", None),
        P("head", "seq", None),
        P("head", None),
        P("head", "seq"),
        P("seq"),
    )
    out_specs = (P("head", "seq", None), P("head", "seq", None), P("head", "seq", None))
    return jax.shard_map(
        per_device, mesh=mesh, in_specs=in_specs, out_specs=out_specs, check_vma=False
    )
```

time: 145 us -> 49.9 us (0.34)
  starting transfers between devices: 58.6 us -> 0 us
  waiting for transfers between devices: 44.9 us -> 0 us
  Pallas kernels: 0 us -> 41.1 us
  between operations: 18.8 us -> 0.66 us
  matrix products: 10.2 us -> 0 us
  local copies, waits for them, and re-layouts: 0.94 us -> 7.92 us
  blocking collectives: 5.66 us -> 0 us
  other arithmetic: 4.45 us -> 0 us
    ppermute x16 -> x0, starting transfers between devices: 58.6 us -> none  [from_behind(): return lax.ppermute(array, axis, pairs)]
    ppermute x16 -> x0, waiting for transfers between devices: 44.9 us -> none  [from_behind(): return lax.ppermute(array, axis, pairs)]
    pallas_call x0 -> x1, Pallas kernels: none -> 41.1 us  [per_device(): pl.pallas_call(functools.partial(body, n, hs), out_shape=(out, out, out),...]
    dot_general x12 -> x0, matrix products: 10.2 us -> none  [product(): jnp.einsum(pattern, left_side, right_side, precision=PRECISE, preferred_e...]
    unnamed x15 -> x17, local copies, waits for them, and re-layouts: 0.17 us -> 7.92 us
    psum x1 -> x0, blocking collectives: 5.66 us -> none  [per_device(): lax.psum((jnp.sum(attended * attended, axis=(0, 2)), jnp.sum(scaled_grad...]
    eq x1 -> x0, other arithmetic: 2.55 us -> none  [per_device(): to_next = jnp.where((labels == arrived_back[2])[None, :], decay_tail, 0.0)]
  transfers between devices with their start and end apart: 16 -> 0, of which waited for: 7 -> 0; matrix products, arithmetic and copies ran while one was open for 4% -> 0% of each run, Pallas kernels for 0% -> 0%
where the time goes in v1:
time: 49.9 us; the launch traced here: 49.6 us
  Pallas kernels  41.1 us (82%)
  local copies, waits for them, and re-layouts  7.92 us (16%)
  between operations  0.66 us (1%)
    pallas_call x1, Pallas kernels, per_device(): pl.pallas_call(functools.partial(body, n, hs), out_shape=(out, out, out),...  41.1 us
    unnamed x17, local copies, waits for them, and re-layouts  7.92 us

profile of v1, /device:TPU:0, one launch (start us, length us, event | category | flops | bytes accessed | tf_op | source)
XLA Modules:
  0.0 49.6 jit_solution(15224515957569069577)
XLA Ops:
  0.6 0.0 copy-start.6
  0.6 0.6 %copy-done.6 = s32[128]{0:T(128)S(1)} copy-done((s32[128]{0:T(128)S(1)}, s32[128]{0:T(128)}, u32[]{:S(2)}) %copy-start.6) | copy-done | bytes 536
  1.3 0.0 copy-start
  1.3 0.9 %copy-done = f32[4,128,128]{2,1,0:T(8,128)S(1)} copy-done((f32[4,128,128]{2,1,0:T(8,128)S(1)}, f32[4,128,128]{2,1,0:T(8,128)}, u32[]{:S(2)}) %copy-start) | copy-done | bytes 262168
  2.2 0.0 copy-start.1
  2.2 0.9 %copy-done.1 = f32[4,128,128]{2,1,0:T(8,128)S(1)} copy-done((f32[4,128,128]{2,1,0:T(8,128)S(1)}, f32[4,128,128]{2,1,0:T(8,128)}, u32[]{:S(2)}) %copy-start.1) | copy-done | bytes 262168
  3.2 0.0 copy-start.2
  3.2 0.9 %copy-done.2 = f32[4,128,128]{2,1,0:T(8,128)S(1)} copy-done((f32[4,128,128]{2,1,0:T(8,128)S(1)}, f32[4,128,128]{2,1,0:T(8,128)}, u32[]{:S(2)}) %copy-start.2) | copy-done | bytes 262168
  4.1 0.0 copy-start.3
  4.1 0.9 %copy-done.3 = f32[4,128,128]{2,1,0:T(8,128)S(1)} copy-done((f32[4,128,128]{2,1,0:T(8,128)S(1)}, f32[4,128,128]{2,1,0:T(8,128)}, u32[]{:S(2)}) %copy-start.3) | copy-done | bytes 262168
  5.1 0.0 copy-start.4
  5.1 0.7 %copy-done.4 = f32[4,128]{1,0:T(4,128)S(1)} copy-done((f32[4,128]{1,0:T(4,128)S(1)}, f32[4,128]{1,0:T(4,128)}, u32[]{:S(2)}) %copy-start.4) | copy-done | bytes 2072
  5.8 0.0 copy-start.5
  5.8 0.7 %copy-done.5 = f32[4,128]{1,0:T(4,128)S(1)} copy-done((f32[4,128]{1,0:T(4,128)S(1)}, f32[4,128]{1,0:T(4,128)}, u32[]{:S(2)}) %copy-start.5) | copy-done | bytes 2072
  6.5 41.1 %shard_map.94 = (f32[4,128,128]{2,1,0:T(8,128)S(1)}, f32[4,128,128]{2,1,0:T(8,128)S(1)}, f32[4,128,128]{2,1,0:T(8,128)S(1)}) custom-call(f32[4,128,128]{2,1,0:T(8,128)S(1)} %copy-done, f32[4,128,128]{2,1,0:T(8,128)S(1)} %copy-done.1, f32[4,128,128]{2,1,0:T(8,128)S(1)} %copy-done.2, f32[4,128,128]{2,1,0:T(8,128)S(1)} %copy-done.3, f32[4,128]{1,0:T(4,128)S(1)} %copy-done.4, ...), custom_call_target="tpu_custom_call" | custom-call | tf_op jit(solution)/shard_map/pallas_call | solution.py:323
  47.5 0.7 %copy.13 = f32[4,128,128]{2,1,0:T(8,128)} copy(f32[4,128,128]{2,1,0:T(8,128)S(1)} %get-tuple-element.6) | data formatting | bytes 524288
  48.2 0.7 %copy.14 = f32[4,128,128]{2,1,0:T(8,128)} copy(f32[4,128,128]{2,1,0:T(8,128)S(1)} %get-tuple-element.7) | data formatting | bytes 524288
  48.9 0.7 %copy.15 = f32[4,128,128]{2,1,0:T(8,128)} copy(f32[4,128,128]{2,1,0:T(8,128)S(1)} %get-tuple-element.8) | data formatting | bytes 524288
Async XLA Ops:
  0.6 0.7 %copy-start.6 = (s32[128]{0:T(128)S(1)}, s32[128]{0:T(128)}, u32[]{:S(2)}) copy-start(s32[128]{0:T(128)} %param.13) | copy-start | bytes 1540
  1.3 0.9 %copy-start = (f32[4,128,128]{2,1,0:T(8,128)S(1)}, f32[4,128,128]{2,1,0:T(8,128)}, u32[]{:S(2)}) copy-start(f32[4,128,128]{2,1,0:T(8,128)} %q.1) | copy-start | bytes 786436
  2.2 0.9 %copy-start.1 = (f32[4,128,128]{2,1,0:T(8,128)S(1)}, f32[4,128,128]{2,1,0:T(8,128)}, u32[]{:S(2)}) copy-start(f32[4,128,128]{2,1,0:T(8,128)} %k.1) | copy-start | bytes 786436
  3.2 0.9 %copy-start.2 = (f32[4,128,128]{2,1,0:T(8,128)S(1)}, f32[4,128,128]{2,1,0:T(8,128)}, u32[]{:S(2)}) copy-start(f32[4,128,128]{2,1,0:T(8,128)} %v.1) | copy-start | bytes 786436
  4.1 0.9 %copy-start.3 = (f32[4,128,128]{2,1,0:T(8,128)S(1)}, f32[4,128,128]{2,1,0:T(8,128)}, u32[]{:S(2)}) copy-start(f32[4,128,128]{2,1,0:T(8,128)} %og.1) | copy-start | bytes 786436
  5.1 0.7 %copy-start.4 = (f32[4,128]{1,0:T(4,128)S(1)}, f32[4,128]{1,0:T(4,128)}, u32[]{:S(2)}) copy-start(f32[4,128]{1,0:T(4,128)} %gain.1) | copy-start | bytes 6148
  5.8 0.7 %copy-start.5 = (f32[4,128]{1,0:T(4,128)S(1)}, f32[4,128]{1,0:T(4,128)}, u32[]{:S(2)}) copy-start(f32[4,128]{1,0:T(4,128)} %ld.1) | copy-start | bytes 6148

commit v2 on v1

--- a/solution.py
+++ b/solution.py
@@ -20,16 +20,20 @@
 
 
 def mm(a, b, dims):
-    def one(x, y):
-        return lax.dot_general(x, y, dims, preferred_element_type=F32)
-
-    return one(a[0], b[0]) + (one(a[0], b[1]) + one(a[1], b[0]))
-
-
-def body(n, hs, q, k, v, og, gain, ld, doc, dq, dk, dv,
+    left = jnp.concatenate([a[0], a[1], a[0]], axis=1)
+    right = jnp.concatenate([b[0], b[0], b[1]], axis=dims[0][1][0])
+    return lax.dot_general(left, right, dims, preferred_element_type=F32)
+
+
+def body(n, hs, q_in, k_in, v_in, og_in, gain_in, ld_in, doc_in, dq, dk, dv,
+         q, k, v, og, gain, ld, doc, in_sem,
          own_f, pair_f, w_f, a_f, b_f, own_b, pair_b, w_b, a_b, b_b,
          att, wgt, wth, prior, ags, tot, send, recv, psend, precv):
     heads, rows, width = q.shape
+    order = ((ld_in, ld), (doc_in, doc), (k_in, k), (v_in, v), (q_in, q), (og_in, og), (gain_in, gain))
+    loads = [pltpu.make_async_copy(a, b, in_sem.at[i]) for i, (a, b) in enumerate(order)]
+    for load in loads:
+        load.start()
     s = lax.axis_index("seq")
     hd = lax.axis_index("head")
     odd_i = lax.rem(s, 2)
@@ -75,6 +79,8 @@
     def d_b(h):
         return copy(5, h, a_b, b_b, s - 2)
 
+    loads[0].wait()
+    loads[1].wait()
     ri = lax.broadcasted_iota(jnp.int32, (rows, rows), 0)
     ci = lax.broadcasted_iota(jnp.int32, (rows, rows), 1)
     tri = jnp.where(ri <= ci, 1.0, 0.0)
@@ -106,6 +112,8 @@
         buf[h, 0:width, :] = state
         buf[h, width:width + 8, :] = meta(passing(h), first, last)
 
+    loads[2].wait()
+    loads[3].wait()
     for h in range(heads):
         tail = jnp.where(lab == last[:, 0:1], jnp.exp(total(h) - row(h)), 0.0)
         put(own_f, h, mm(split(k[h].T * tail), split(v[h]), NN))
@@ -187,6 +195,8 @@
         return attended * attended, scaled * attended
 
     half = heads // 2
+    for load in loads[4:]:
+        load.wait()
     for h in range(half):
         local_forward(h)
     for h in range(heads):
@@ -323,9 +333,12 @@
     return pl.pallas_call(
         functools.partial(body, n, hs),
         out_shape=(out, out, out),
-        in_specs=[whole] * 7,
+        in_specs=[pl.BlockSpec(memory_space=pltpu.MemorySpace.HBM)] * 7,
         out_specs=(whole, whole, whole),
-        scratch_shapes=[state] * 10 + [
+        scratch_shapes=[square] * 4 + [
+            pltpu.VMEM(norm_gain.shape, F32), pltpu.VMEM(log_decay.shape, F32),
+            pltpu.VMEM((1, rows), jnp.int32), pltpu.SemaphoreType.DMA((7,)),
+        ] + [state] * 10 + [
             square, scores, scores, pltpu.VMEM((heads, width, width), F32), square,
             pltpu.VMEM((hs, 8, rows), F32),
             pltpu.SemaphoreType.DMA((6, heads)), pltpu.SemaphoreType.DMA((6, heads)),

time: 49.9 us -> 50.1 us (level)
  no operation moved by 1% of the time
where the time goes in v2:
time: 50.1 us; the launch traced here: 49.8 us
  Pallas kernels  41.2 us (82%)
  local copies, waits for them, and re-layouts  7.92 us (16%)
  between operations  0.66 us (1%)
    pallas_call x1, Pallas kernels, per_device(): pl.pallas_call(functools.partial(body, n, hs), out_shape=(out, out, out),...  41.2 us
    unnamed x17, local copies, waits for them, and re-layouts  7.92 us

profile of v2, /device:TPU:0, one launch (start us, length us, event | category | flops | bytes accessed | tf_op | source)
XLA Modules:
  0.0 49.8 jit_solution(12985548894940135678)
XLA Ops:
  0.6 0.0 copy-start.6
  0.6 0.6 %copy-done.6 = s32[128]{0:T(128)S(1)} copy-done((s32[128]{0:T(128)S(1)}, s32[128]{0:T(128)}, u32[]{:S(2)}) %copy-start.6) | copy-done | bytes 536
  1.3 0.0 copy-start
  1.3 0.9 %copy-done = f32[4,128,128]{2,1,0:T(8,128)S(1)} copy-done((f32[4,128,128]{2,1,0:T(8,128)S(1)}, f32[4,128,128]{2,1,0:T(8,128)}, u32[]{:S(2)}) %copy-start) | copy-done | bytes 262168
  2.2 0.0 copy-start.1
  2.2 0.9 %copy-done.1 = f32[4,128,128]{2,1,0:T(8,128)S(1)} copy-done((f32[4,128,128]{2,1,0:T(8,128)S(1)}, f32[4,128,128]{2,1,0:T(8,128)}, u32[]{:S(2)}) %copy-start.1) | copy-done | bytes 262168
  3.2 0.0 copy-start.2
  3.2 0.9 %copy-done.2 = f32[4,128,128]{2,1,0:T(8,128)S(1)} copy-done((f32[4,128,128]{2,1,0:T(8,128)S(1)}, f32[4,128,128]{2,1,0:T(8,128)}, u32[]{:S(2)}) %copy-start.2) | copy-done | bytes 262168
  4.1 0.0 copy-start.3
  4.1 0.9 %copy-done.3 = f32[4,128,128]{2,1,0:T(8,128)S(1)} copy-done((f32[4,128,128]{2,1,0:T(8,128)S(1)}, f32[4,128,128]{2,1,0:T(8,128)}, u32[]{:S(2)}) %copy-start.3) | copy-done | bytes 262168
  5.1 0.0 copy-start.4
  5.1 0.7 %copy-done.4 = f32[4,128]{1,0:T(4,128)S(1)} copy-done((f32[4,128]{1,0:T(4,128)S(1)}, f32[4,128]{1,0:T(4,128)}, u32[]{:S(2)}) %copy-start.4) | copy-done | bytes 2072
  5.8 0.0 copy-start.5
  5.8 0.7 %copy-done.5 = f32[4,128]{1,0:T(4,128)S(1)} copy-done((f32[4,128]{1,0:T(4,128)S(1)}, f32[4,128]{1,0:T(4,128)}, u32[]{:S(2)}) %copy-start.5) | copy-done | bytes 2072
  6.5 41.2 %shard_map.94 = (f32[4,128,128]{2,1,0:T(8,128)S(1)}, f32[4,128,128]{2,1,0:T(8,128)S(1)}, f32[4,128,128]{2,1,0:T(8,128)S(1)}) custom-call(f32[4,128,128]{2,1,0:T(8,128)S(1)} %copy-done, f32[4,128,128]{2,1,0:T(8,128)S(1)} %copy-done.1, f32[4,128,128]{2,1,0:T(8,128)S(1)} %copy-done.2, f32[4,128,128]{2,1,0:T(8,128)S(1)} %copy-done.3, f32[4,128]{1,0:T(4,128)S(1)} %copy-done.4, ...), custom_call_target="tpu_custom_call" | custom-call | tf_op jit(solution)/shard_map/pallas_call | solution.py:333
  47.7 0.7 %copy.13 = f32[4,128,128]{2,1,0:T(8,128)} copy(f32[4,128,128]{2,1,0:T(8,128)S(1)} %get-tuple-element.6) | data formatting | bytes 524288
  48.4 0.7 %copy.14 = f32[4,128,128]{2,1,0:T(8,128)} copy(f32[4,128,128]{2,1,0:T(8,128)S(1)} %get-tuple-element.7) | data formatting | bytes 524288
  49.1 0.7 %copy.15 = f32[4,128,128]{2,1,0:T(8,128)} copy(f32[4,128,128]{2,1,0:T(8,128)S(1)} %get-tuple-element.8) | data formatting | bytes 524288
Async XLA Ops:
  0.6 0.7 %copy-start.6 = (s32[128]{0:T(128)S(1)}, s32[128]{0:T(128)}, u32[]{:S(2)}) copy-start(s32[128]{0:T(128)} %param.13) | copy-start | bytes 1540
  1.3 0.9 %copy-start = (f32[4,128,128]{2,1,0:T(8,128)S(1)}, f32[4,128,128]{2,1,0:T(8,128)}, u32[]{:S(2)}) copy-start(f32[4,128,128]{2,1,0:T(8,128)} %q_in.1) | copy-start | bytes 786436
  2.2 0.9 %copy-start.1 = (f32[4,128,128]{2,1,0:T(8,128)S(1)}, f32[4,128,128]{2,1,0:T(8,128)}, u32[]{:S(2)}) copy-start(f32[4,128,128]{2,1,0:T(8,128)} %k_in.1) | copy-start | bytes 786436
  3.2 0.9 %copy-start.2 = (f32[4,128,128]{2,1,0:T(8,128)S(1)}, f32[4,128,128]{2,1,0:T(8,128)}, u32[]{:S(2)}) copy-start(f32[4,128,128]{2,1,0:T(8,128)} %v_in.1) | copy-start | bytes 786436
  4.1 0.9 %copy-start.3 = (f32[4,128,128]{2,1,0:T(8,128)S(1)}, f32[4,128,128]{2,1,0:T(8,128)}, u32[]{:S(2)}) copy-start(f32[4,128,128]{2,1,0:T(8,128)} %og_in.1) | copy-start | bytes 786436
  5.1 0.7 %copy-start.4 = (f32[4,128]{1,0:T(4,128)S(1)}, f32[4,128]{1,0:T(4,128)}, u32[]{:S(2)}) copy-start(f32[4,128]{1,0:T(4,128)} %gain_in.1) | copy-start | bytes 6148
  5.8 0.7 %copy-start.5 = (f32[4,128]{1,0:T(4,128)S(1)}, f32[4,128]{1,0:T(4,128)}, u32[]{:S(2)}) copy-start(f32[4,128]{1,0:T(4,128)} %ld_in.1) | copy-start | bytes 6148

commit v3 on v2

--- a/solution.py
+++ b/solution.py
@@ -346,7 +346,8 @@
         ],
         compiler_params=pltpu.CompilerParams(
             collective_id=0, has_side_effects=True, vmem_limit_bytes=32 * 1024 * 1024),
-    )(queries, keys, values, out_grad, norm_gain, log_decay, doc_ids[None, :])
+    )(*[pltpu.with_memory_space_constraint(x, pltpu.MemorySpace.HBM) for x in
+        (queries, keys, values, out_grad, norm_gain, log_decay, doc_ids[None, :])])
 
 
 def solution(mesh):

time: 50.1 us -> 44.1 us (0.88)
  local copies, waits for them, and re-layouts: 7.92 us -> 2.11 us
    unnamed x17 -> x3, local copies, waits for them, and re-layouts: 7.92 us -> 2.11 us
where the time goes in v3:
time: 44.1 us; the launch traced here: 43.9 us
  Pallas kernels  41.1 us (93%)
  local copies, waits for them, and re-layouts  2.11 us (5%)
  between operations  0.64 us (1%)
    pallas_call x1, Pallas kernels, per_device(): pl.pallas_call(functools.partial(body, n, hs), out_shape=(out, out, out),...  41.1 us
    unnamed x3, local copies, waits for them, and re-layouts  2.11 us

profile of v3, /device:TPU:0, one launch (start us, length us, event | category | flops | bytes accessed | tf_op | source)
XLA Modules:
  0.0 43.9 jit_solution(15264392772279820548)
XLA Ops:
  0.6 41.1 %shard_map.94 = (f32[4,128,128]{2,1,0:T(8,128)S(1)}, f32[4,128,128]{2,1,0:T(8,128)S(1)}, f32[4,128,128]{2,1,0:T(8,128)S(1)}) custom-call(f32[4,128,128]{2,1,0:T(8,128)} %q_in.1, f32[4,128,128]{2,1,0:T(8,128)} %k_in.1, f32[4,128,128]{2,1,0:T(8,128)} %v_in.1, f32[4,128,128]{2,1,0:T(8,128)} %og_in.1, f32[4,128]{1,0:T(4,128)} %gain_in.1, f32[4,128]{1,0:T(4,128)} %ld_in.1, ...), custom_call_target="tpu_custom_call" | custom-call | tf_op jit(solution)/shard_map/pallas_call | solution.py:333
  41.8 0.7 %copy.13 = f32[4,128,128]{2,1,0:T(8,128)} copy(f32[4,128,128]{2,1,0:T(8,128)S(1)} %get-tuple-element.6) | data formatting | bytes 524288
  42.5 0.7 %copy.14 = f32[4,128,128]{2,1,0:T(8,128)} copy(f32[4,128,128]{2,1,0:T(8,128)S(1)} %get-tuple-element.7) | data formatting | bytes 524288
  43.2 0.7 %copy.15 = f32[4,128,128]{2,1,0:T(8,128)} copy(f32[4,128,128]{2,1,0:T(8,128)S(1)} %get-tuple-element.8) | data formatting | bytes 524288

commit v4 on v3

--- a/solution.py
+++ b/solution.py
@@ -201,9 +201,11 @@
         local_forward(h)
     for h in range(heads):
         merge_forward(h)
-    for h in range(half, heads):
-        local_forward(h)
-    for h in range(heads):
+        if h % 2 == 0 and half + h // 2 < heads:
+            local_forward(half + h // 2)
+        if h >= 2:
+            relay_forward(h - 2)
+    for h in range(max(heads - 2, 0), heads):
         relay_forward(h)
     squares, inner = None, None
     for h in range(heads):
@@ -295,9 +297,11 @@
         local_backward(h)
     for h in range(heads):
         merge_backward(h)
-    for h in range(half, heads):
-        local_backward(h)
-    for h in range(heads):
+        if h % 2 == 0 and half + h // 2 < heads:
+            local_backward(half + h // 2)
+        if h >= 2:
+            relay_backward(h - 2)
+    for h in range(max(heads - 2, 0), heads):
         relay_backward(h)
     for h in range(heads):
         finish_backward(h)

time: 44.1 us -> 45.6 us (1.034)
  Pallas kernels: 41.1 us -> 42.6 us
    pallas_call x1, Pallas kernels: 41.1 us -> 42.6 us  [per_device(): pl.pallas_call(functools.partial(body, n, hs), out_shape=(out, out, out),...]
where the time goes in v4:
time: 45.6 us; the launch traced here: 45.4 us
  Pallas kernels  42.6 us (93%)
  local copies, waits for them, and re-layouts  2.11 us (5%)
  between operations  0.64 us (1%)
    pallas_call x1, Pallas kernels, per_device(): pl.pallas_call(functools.partial(body, n, hs), out_shape=(out, out, out),...  42.6 us
    unnamed x3, local copies, waits for them, and re-layouts  2.11 us

profile of v4, /device:TPU:0, one launch (start us, length us, event | category | flops | bytes accessed | tf_op | source)
XLA Modules:
  0.0 45.4 jit_solution(2684534375824738656)
XLA Ops:
  0.6 42.6 %shard_map.94 = (f32[4,128,128]{2,1,0:T(8,128)S(1)}, f32[4,128,128]{2,1,0:T(8,128)S(1)}, f32[4,128,128]{2,1,0:T(8,128)S(1)}) custom-call(f32[4,128,128]{2,1,0:T(8,128)} %q_in.1, f32[4,128,128]{2,1,0:T(8,128)} %k_in.1, f32[4,128,128]{2,1,0:T(8,128)} %v_in.1, f32[4,128,128]{2,1,0:T(8,128)} %og_in.1, f32[4,128]{1,0:T(4,128)} %gain_in.1, f32[4,128]{1,0:T(4,128)} %ld_in.1, ...), custom_call_target="tpu_custom_call" | custom-call | tf_op jit(solution)/shard_map/pallas_call | solution.py:337
  43.3 0.7 %copy.13 = f32[4,128,128]{2,1,0:T(8,128)} copy(f32[4,128,128]{2,1,0:T(8,128)S(1)} %get-tuple-element.6) | data formatting | bytes 524288
  44.0 0.7 %copy.14 = f32[4,128,128]{2,1,0:T(8,128)} copy(f32[4,128,128]{2,1,0:T(8,128)S(1)} %get-tuple-element.7) | data formatting | bytes 524288
  44.7 0.7 %copy.15 = f32[4,128,128]{2,1,0:T(8,128)} copy(f32[4,128,128]{2,1,0:T(8,128)S(1)} %get-tuple-element.8) | data formatting | bytes 524288
